TPU v7x, 32 devices: a whole 2x2x4 slice. The times are simulated.
32 devices in a mesh: ep: 16 (over z, y, x), dp: 2 (over core).
Axes of the slice: x: 2, y: 2, z: 4, core: 2. Of those that a mesh axis runs over, the one named last changes fastest.
Arguments:
- layer_input: bfloat16 [2048, 3584], P('ep'), may hold values from -6 to 6
- out_grad: bfloat16 [2048, 3584], P('ep'), may hold values from -6 to 6
- expert_ids: int32 [2048, 8], P('ep'), may hold values from 0 to 15, all different within a row; in each aligned block of 128 rows (0 to 127, 128 to 255, ...) at most 80 rows name the same one
- gate_probs: float32 [2048, 8], P('ep'), may hold values from 0.1 to 1
- gate_proj: bfloat16 [16, 3584, 1024], P('ep'), may hold values from -0.09375 to 0.09375
- up_proj: bfloat16 [16, 3584, 1024], P('ep'), may hold values from -0.09375 to 0.09375
- down_proj: bfloat16 [16, 1024, 3584], P('ep'), may hold values from -0.1875 to 0.1875
Outputs:
- input_grad: bfloat16 [2048, 3584], P('ep', 'dp')
Inputs may be any that keep to these rules, and one draw needn't show every extreme that they name: `expert_ids`: each row names 8 different experts. The 128 rows of one device name one expert at most 80 times, and in every draw some device's rows name some expert exactly 80 times.
All inputs are finite; a program needn't handle non-finite values.
Results may differ from a plain program's by a relative error of at most 0.0058.
Values may be sent and summed in bfloat16 or wider, within the bound.
A program may use at most 192 MiB of HBM per device.

v0:
```python
import functools

import jax
import jax.numpy as jnp
from jax import lax
from jax.experimental import pallas as pl
from jax.experimental.pallas import tpu as pltpu
from jax.sharding import PartitionSpec as P

MESH = pl.DeviceIdType.MESH
NT = (((1,), (1,)), ((), ()))


def flipped(z, j, planes):
    result, bit = z, 1
    while bit < planes:
        if j & bit:
            result = result + bit * (1 - 2 * ((z // bit) % 2))
        bit *= 2
    return result


def kernel(planes, x_hbm, g_hbm, w_ref, wg_hbm, wu_hbm, wd_hbm, out_ref,
           data, part, wgv, wuv, wdv, gg, ug, r1a, r1b, r2x, r2y, r3, fin,
           send_sem, recv_sem, load_sem):
    me, core = lax.axis_index("ep"), lax.axis_index("dp")
    z, y, x = me // 4, (me // 2) % 2, me % 2
    half, features = r2x.shape[1], r2x.shape[2]
    hidden = wgv.shape[1]
    cut = features // 2
    peer_x, peer_y = z * 4 + y * 2 + (1 - x), z * 4 + (1 - y) * 2 + x
    zs = [flipped(z, j, planes) for j in range(planes)]
    peer_z = [zs[j] * 4 + y * 2 + x for j in range(planes)]

    def block(j, dy, dx):
        by = (1 - y) if dy else y
        bx = (1 - x) if dx else x
        return pl.ds(pl.multiple_of((zs[j] * 4 + by * 2 + bx) * half, half), half)

    kinds = ("agz", "agx", "agy", "fa", "fb", "r1a", "r1b", "r2x", "r2y", "r3")
    sent = []

    def number(kind, j):
        return len(kinds) * planes if kind == "dp" else kinds.index(kind) * planes + j

    def send(kind, j, src, dst, to):
        n = number(kind, j)
        copy = pltpu.make_async_remote_copy(
            src_ref=src, dst_ref=dst, send_sem=send_sem.at[n], recv_sem=recv_sem.at[n],
            device_id=to, device_id_type=MESH,
        )
        copy.start()
        sent.append(copy)

    def arrive(kind, j, dst, to):
        n = number(kind, j)
        pltpu.make_async_remote_copy(
            src_ref=dst, dst_ref=dst, send_sem=send_sem.at[n], recv_sem=recv_sem.at[n],
            device_id=to, device_id_type=MESH,
        ).wait_recv()

    to_x, to_y, to_core = {"ep": peer_x}, {"ep": peer_y}, {"dp": 1 - core}
    own = block(0, 0, 0)
    mine = pl.ds(pl.multiple_of(core * half, half), half)
    first = [
        pltpu.make_async_copy(x_hbm.at[mine], data.at[0, own], load_sem.at[0]),
        pltpu.make_async_copy(g_hbm.at[mine], data.at[1, own], load_sem.at[1]),
    ]
    loads = [
        pltpu.make_async_copy(wg_hbm.at[0], wgv, load_sem.at[2]),
        pltpu.make_async_copy(wu_hbm.at[0], wuv, load_sem.at[3]),
        pltpu.make_async_copy(wd_hbm.at[0], wdv, load_sem.at[4]),
    ]
    for copy in first + loads:
        copy.start()

    barrier = pltpu.get_barrier_semaphore()
    greeted = [to_x, to_y, to_core] + [{"ep": peer_z[j]} for j in range(1, planes)]
    for other in greeted:
        pl.semaphore_signal(barrier, inc=1, device_id=other, device_id_type=MESH)
    pl.semaphore_wait(barrier, len(greeted))
    for copy in first:
        copy.wait()

    def gather(j):
        here = data.at[:, block(j, 0, 0), :]
        if j > 0:
            arrive("agz", j, here, {"ep": peer_z[j]})
        send("agx", j, here, here, to_x)
        send("agy", j, here, here, to_y)
        if j == 0:
            for i in range(1, planes):
                send("agz", i, here, here, {"ep": peer_z[i]})

    def forward(j):
        from_x = block(j, 0, 1)
        arrive("agx", j, data.at[:, from_x, :], to_x)
        piece = data.at[:, from_x, pl.ds(0, cut)]
        send("fa", j, piece, piece, to_y)
        from_y = block(j, 1, 0)
        arrive("agy", j, data.at[:, from_y, :], to_y)
        piece = data.at[:, from_y, pl.ds(cut, cut)]
        send("fb", j, piece, piece, to_x)

    def compute(j):
        far = block(j, 1, 1)
        arrive("fa", j, data.at[:, far, pl.ds(0, cut)], to_y)
        arrive("fb", j, data.at[:, far, pl.ds(cut, cut)], to_x)
        rows = pl.ds(pl.multiple_of(zs[j] * 4 * half, 4 * half), 4 * half)
        tile = 256

        @pl.loop(0, hidden // tile)
        def _(f):
            cols = pl.ds(pl.multiple_of(f * tile, tile), tile)
            tokens = data[0, rows, :]
            gate = jnp.dot(tokens, wgv[:, cols], preferred_element_type=jnp.float32)
            up = jnp.dot(tokens, wuv[:, cols], preferred_element_type=jnp.float32)
            grad = lax.dot_general(data[1, rows, :], wdv[cols, :], NT, preferred_element_type=jnp.float32)
            s = jax.nn.sigmoid(gate)
            gg[:, cols] = (grad * up * s * (1.0 + gate * (1.0 - s))).astype(jnp.bfloat16)
            ug[:, cols] = (grad * gate * s).astype(jnp.bfloat16)

        wide = 512

        @pl.loop(0, features // wide)
        def _(d):
            cols = pl.ds(pl.multiple_of(d * wide, wide), wide)
            back = lax.dot_general(gg[...], wgv[cols, :], NT, preferred_element_type=jnp.float32)
            back = back + lax.dot_general(ug[...], wuv[cols, :], NT, preferred_element_type=jnp.float32)
            part[rows, cols] = (back * w_ref[rows, :]).astype(jnp.bfloat16)

    def reduce1(j):
        far = block(j, 1, 1)
        send("r1a", j, part.at[far, pl.ds(0, cut)], r1a.at[j], to_y)
        send("r1b", j, part.at[far, pl.ds(cut, cut)], r1b.at[j], to_x)

    def reduce2(j):
        side = block(j, 0, 1)
        arrive("r1a", j, r1a.at[j], to_y)
        part[side, 0:cut] = (part[side, 0:cut].astype(jnp.float32) + r1a[j].astype(jnp.float32)).astype(jnp.bfloat16)
        send("r2x", j, part.at[side], r2x.at[j], to_x)
        side = block(j, 1, 0)
        arrive("r1b", j, r1b.at[j], to_x)
        part[side, cut:] = (part[side, cut:].astype(jnp.float32) + r1b[j].astype(jnp.float32)).astype(jnp.bfloat16)
        send("r2y", j, part.at[side], r2y.at[j], to_y)

    def reduce3(j):
        here = block(j, 0, 0)
        arrive("r2x", j, r2x.at[j], to_x)
        arrive("r2y", j, r2y.at[j], to_y)
        if j > 0:
            total = part[here, :].astype(jnp.float32) + r2x[j].astype(jnp.float32) + r2y[j].astype(jnp.float32)
            part[here, :] = total.astype(jnp.bfloat16)
            send("r3", j, part.at[here], r3.at[j], {"ep": peer_z[j]})

    steps = [(gather, 0), (forward, 0), (gather, 1)]
    for j in range(planes):
        if j == 0:
            for copy in loads:
                steps.append((lambda _, c=copy: c.wait(), 0))
        steps += [(compute, j), (reduce1, j)]
        if j + 1 < planes:
            steps.append((forward, j + 1))
        if j + 2 < planes:
            steps.append((gather, j + 2))
        if j >= 1:
            steps.append((reduce3, j - 1))
        steps.append((reduce2, j))
    steps.append((reduce3, planes - 1))
    for step, j in steps:
        step(j)

    for j in range(1, planes):
        arrive("r3", j, r3.at[j], {"ep": peer_z[j]})
    for h in range(2):
        cols = slice(h * cut, (h + 1) * cut)
        total = part[own, cols].astype(jnp.float32)
        total = total + r2x[0, :, cols].astype(jnp.float32) + r2y[0, :, cols].astype(jnp.float32)
        for j in range(1, planes):
            total = total + r3[j, :, cols].astype(jnp.float32)
        fin[h] = total.astype(jnp.bfloat16)
    keep = pltpu.make_async_copy(fin.at[core], out_ref.at[mine], load_sem.at[5])
    keep.start()
    send("dp", 0, fin.at[1 - core], out_ref.at[mine], to_core)
    theirs = pl.ds(pl.multiple_of((1 - core) * half, half), half)
    arrive("dp", 0, out_ref.at[theirs], to_core)
    keep.wait()
    for copy in sent:
        copy.wait_send()


def weights_of(expert_ids, gate_probs, experts, half, core):
    ids = lax.dynamic_slice_in_dim(expert_ids, core * half, half, 0)
    probs = lax.dynamic_slice_in_dim(gate_probs, core * half, half, 0)
    names = jnp.arange(experts, dtype=jnp.int32)
    table = jnp.sum(
        jnp.where(ids[None, :, :] == names[:, None, None], probs[None, :, :], 0.0), axis=2
    )
    return lax.all_to_all(table, "ep", split_axis=0, concat_axis=0, tiled=True).reshape(-1)


def fused(layer_input, out_grad, expert_ids, gate_probs, gate_proj, up_proj, down_proj):
    experts, halves = lax.axis_size("ep"), lax.axis_size("dp")
    tok_rows, features = layer_input.shape
    hidden = gate_proj.shape[2]
    half = tok_rows // halves
    planes = experts // 4
    weight = weights_of(expert_ids, gate_probs, experts, half, lax.axis_index("dp"))
    rows, cut, bf16 = experts * half, features // 2, jnp.bfloat16
    vmem, hbm = pl.BlockSpec(memory_space=pltpu.VMEM), pl.BlockSpec(memory_space=pl.ANY)
    count = 10 * planes + 1
    return pl.pallas_call(
        functools.partial(kernel, planes),
        name="fused_backward",
        out_shape=jax.ShapeDtypeStruct((tok_rows, features // halves), bf16),
        in_specs=[hbm, hbm, vmem, hbm, hbm, hbm],
        out_specs=vmem,
        scratch_shapes=[
            pltpu.VMEM((2, rows, features), bf16),
            pltpu.VMEM((rows, features), bf16),
            pltpu.VMEM((features, hidden), bf16),
            pltpu.VMEM((features, hidden), bf16),
            pltpu.VMEM((hidden, features), bf16),
            pltpu.VMEM((4 * half, hidden), bf16),
            pltpu.VMEM((4 * half, hidden), bf16),
            pltpu.VMEM((planes, half, cut), bf16),
            pltpu.VMEM((planes, half, cut), bf16),
            pltpu.VMEM((planes, half, features), bf16),
            pltpu.VMEM((planes, half, features), bf16),
            pltpu.VMEM((planes, half, features), bf16),
            pltpu.VMEM((halves, half, cut), bf16),
            pltpu.SemaphoreType.DMA((count,)),
            pltpu.SemaphoreType.DMA((count,)),
            pltpu.SemaphoreType.DMA((6,)),
        ],
        compiler_params=pltpu.CompilerParams(
            collective_id=0, has_side_effects=True, vmem_limit_bytes=67043328
        ),
    )(layer_input, out_grad, weight[:, None], gate_proj, up_proj, down_proj)


def dense(layer_input, out_grad, expert_ids, gate_probs, gate_proj, up_proj, down_proj):
    experts = lax.axis_size("ep")
    halves = lax.axis_size("dp")
    tok_rows, features = layer_input.shape
    half = tok_rows // halves
    core = lax.axis_index("dp")
    start = core * half
    mine_in = lax.dynamic_slice_in_dim(layer_input, start, half, 0)
    mine_grad = lax.dynamic_slice_in_dim(out_grad, start, half, 0)
    ids = lax.dynamic_slice_in_dim(expert_ids, start, half, 0)
    probs = lax.dynamic_slice_in_dim(gate_probs, start, half, 0)
    names = jnp.arange(experts, dtype=jnp.int32)
    table = jnp.sum(
        jnp.where(ids[None, :, :] == names[:, None, None], probs[None, :, :], 0.0), axis=2
    )
    weight = lax.all_to_all(table, "ep", split_axis=0, concat_axis=0, tiled=True).reshape(-1)
    in_rows = lax.all_gather(mine_in, "ep", axis=0, tiled=True)
    grad_rows = lax.all_gather(mine_grad, "ep", axis=0, tiled=True)
    gate_mat, up_mat, down_mat = (gate_proj[0], up_proj[0], down_proj[0])
    nt = (((1,), (1,)), ((), ()))
    gate_pre = jnp.dot(in_rows, gate_mat, preferred_element_type=jnp.float32)
    up_pre = jnp.dot(in_rows, up_mat, preferred_element_type=jnp.float32)
    hidden_grad = lax.dot_general(grad_rows, down_mat, nt, preferred_element_type=jnp.float32)
    s = jax.nn.sigmoid(gate_pre)
    gate_grad = (hidden_grad * up_pre * s * (1.0 + gate_pre * (1.0 - s))).astype(jnp.bfloat16)
    up_grad = (hidden_grad * gate_pre * s).astype(jnp.bfloat16)
    back = lax.dot_general(gate_grad, gate_mat, nt, preferred_element_type=jnp.float32)
    back = back + lax.dot_general(up_grad, up_mat, nt, preferred_element_type=jnp.float32)
    back = (back * weight[:, None]).astype(jnp.bfloat16)
    mine = lax.psum_scatter(back, "ep", scatter_dimension=0, tiled=True)
    return lax.all_to_all(mine, "dp", split_axis=1, concat_axis=0, tiled=True)


def body(*args):
    experts, halves = lax.axis_size("ep"), lax.axis_size("dp")
    tok_rows, features = args[0].shape
    hidden = args[4].shape[2]
    rows = experts * tok_rows // halves
    held = 2 * features * (3 * rows + 3 * hidden + rows)
    fits = held < 58 * 2**20 and halves == 2 and experts % 4 == 0
    return (fused if fits else dense)(*args)


def solution(mesh):
    row = P("ep", None)
    mat = P("ep", None, None)
    return jax.shard_map(
        body, mesh=mesh, in_specs=(row, row, row, row, mat, mat, mat), out_specs=P("ep", "dp"), check_vma=False
    )
```

profile of v0, /device:TPU:17, one launch (start us, length us, event | category | flops | bytes accessed | tf_op | source)
XLA Modules:
  0.0 232.3 jit_solution(7633229938689487585)
XLA Ops:
  0.0 0.8 constant_dynamic-slice_fusion.1
  0.8 0.8 constant_dynamic-slice_fusion
  1.5 10.5 %all_to_all.9 = f32[16,1,64]{2,1,0:T(1,128)S(1)} all-to-all(f32[16,1,64]{2,1,0:T(1,128)S(1)} %bitcast.3), channel_id=1, replica_groups=mesh['ep'=16,'dp'=2] {'ep'}, dimensions={0} | all-to-all | bytes 8192 | tf_op jit(solution)/shard_map/all_to_all | solution.py:199
  12.1 0.5 broadcast.5
  12.6 0.7 reduce.3
  13.3 1.3 broadcast_in_dim_reshape.4.w_ref
  14.5 215.9 %fused_backward.1 = bf16[128,1792]{1,0:T(8,128)(2,1)} custom-call(bf16[128,3584]{1,0:T(8,128)(2,1)} %x_hbm.1, bf16[128,3584]{1,0:T(8,128)(2,1)} %g_hbm.1, f32[1024,1]{1,0:T(8,128)} %broadcast_in_dim_reshape.4.w_ref, bf16[1,3584,1024]{2,1,0:T(8,128)(2,1)} %wg_hbm.1, bf16[1,3584,1024]{2,1,0:T(8,128)(2,1)} %wu_hbm.1, bf16[1,1024,3584]{2,1,0:T(8,128)(2,1)} %wd_hbm.1), custom_call_target="tpu_custom_call" | custom-call | tf_op jit(solution)/shard_map/fused_backward/pallas_call | solution.py:212
  230.5 1.8 copy.19
  (1 shorter events, 0.0 us)
where the time goes:
time: 233 us; the launch traced here: 232 us
  Pallas kernels  216 us (93%)
  blocking collectives  10.5 us (5%)
  local copies, waits for them, and re-layouts  5.1 us (2%)
    pallas_call x1, Pallas kernels, fused(): pl.pallas_call(functools.partial(kernel, planes), name='fused_backward',...  216 us
    all_to_all x1, blocking collectives, weights_of(): lax.all_to_all(table, 'ep', split_axis=0, concat_axis=0, tiled=True)  10.5 us

commit v1 on v0

v1 whole, which is shorter than its diff:
```python
import functools

import jax
import jax.numpy as jnp
from jax import lax
from jax.experimental import pallas as pl
from jax.experimental.pallas import tpu as pltpu
from jax.sharding import PartitionSpec as P

MESH = pl.DeviceIdType.MESH
NT = (((1,), (1,)), ((), ()))


def kernel(cap, x_hbm, g_hbm, ids_ref, prob_ref, wg_hbm, wu_hbm, wd_hbm, out_ref,
           raw, tabs, stage, comp, part, rc, rr, total, r3, sel, selt, wgv, wuv, wdv, gg, ug, pw, fin,
           send_sem, recv_sem, load_sem):
    me, core = lax.axis_index("ep"), lax.axis_index("dp")
    z, y, x = me // 4, (me // 2) % 2, me % 2
    planes, rows, features = raw.shape[0], raw.shape[2], raw.shape[3]
    hidden, experts = wgv.shape[1], tabs.shape[2] // 2
    cut = features // 2
    f32, bf16 = jnp.float32, jnp.bfloat16
    ad = core == (x + y) % 2
    bc = core != (x + y) % 2
    off1 = jnp.where(ad, 0, cap)
    tab1 = jnp.where(ad, 0, 1)
    inner = (z % (planes - 1)) != 0
    outer = (z % (planes - 1)) == 0
    far = z // 2
    source = [z, z + 1 - 2 * (z % 2), 2 - far, 3 * (1 - far)]
    peer_x, peer_y = z * 4 + y * 2 + (1 - x), z * 4 + (1 - y) * 2 + x
    to_x, to_y, to_core = {"ep": peer_x}, {"ep": peer_y}, {"dp": 1 - core}
    column = [{"ep": s * 4 + y * 2 + x} for s in source]
    above = {"ep": jnp.minimum(z + 1, planes - 1) * 4 + y * 2 + x}
    below = {"ep": jnp.maximum(z - 1, 0) * 4 + y * 2 + x}
    h0, h1 = pl.ds(0, cut), pl.ds(cut, cut)
    lo, hi = pl.ds(0, cap), pl.ds(cap, cap)
    own1 = pl.ds(pl.multiple_of(off1, 16), cap)
    other1 = pl.ds(pl.multiple_of(cap - off1, 16), cap)

    kinds = ("ru", "rd", "tu", "td", "rx", "ry", "tx", "ty", "t2", "sx", "sy", "px", "py", "qx", "qy", "zz", "dp")
    sent, staged = [], {}

    def number(kind, i):
        return kinds.index(kind) * planes + i

    def make(kind, i, src, dst, to, got=None):
        return pltpu.make_async_remote_copy(
            src_ref=src, dst_ref=dst, send_sem=send_sem.at[number(kind, i)],
            recv_sem=recv_sem.at[number(kind, i if got is None else got)],
            device_id=to, device_id_type=MESH,
        )

    def send(cond, kind, i, ends, to, got=None):
        make(kind, i, *ends(), to, got).start()
        done = lambda: make(kind, i, *ends(), to, got).wait_send()
        if kind in ("sx", "sy"):
            staged[kind, i] = done
        else:
            sent.append((cond, done))

    def arrive(kind, i, dst, to):
        make(kind, i, dst, dst, to).wait_recv()

    def when(cond, body):
        pl.when(cond)(body)

    loads = [
        pltpu.make_async_copy(wg_hbm.at[0], wgv, load_sem.at[2]),
        pltpu.make_async_copy(wu_hbm.at[0], wuv, load_sem.at[3]),
        pltpu.make_async_copy(wd_hbm.at[0], wdv, load_sem.at[4]),
    ]

    def own_copies():
        return [
            pltpu.make_async_copy(x_hbm, raw.at[z, 0], load_sem.at[0]),
            pltpu.make_async_copy(g_hbm, raw.at[z, 1], load_sem.at[1]),
        ]

    def begin():
        for copy in own_copies():
            copy.start()

    when(ad, begin)
    for copy in loads:
        copy.start()

    barrier = pltpu.get_barrier_semaphore()
    greeted = [to_x, to_y, to_core]
    greeted += column[1:]
    for other in greeted:
        pl.semaphore_signal(barrier, inc=1, device_id=other, device_id_type=MESH)

    def table():
        name = lax.broadcasted_iota(jnp.int32, (rows, 128), 1)
        count = jnp.zeros((rows, 128), f32)
        prob = jnp.zeros((rows, 128), f32)
        for k in range(ids_ref.shape[1]):
            hit = ids_ref[:, k:k + 1] == name
            count = count + jnp.where(hit, 1.0, 0.0)
            prob = prob + jnp.where(hit, prob_ref[:, k:k + 1], 0.0)
        before = lax.broadcasted_iota(jnp.int32, (rows, rows), 1) < lax.broadcasted_iota(jnp.int32, (rows, rows), 0)
        lower = jnp.where(before, 1.0, 0.0).astype(bf16)
        rank = jnp.dot(lower, count.astype(bf16), preferred_element_type=f32)
        code = jnp.where(count > 0.5, rank, -1.0)
        tabs[z, 0, 0:experts, :] = code.T[0:experts]
        tabs[z, 0, experts:, :] = prob.T[0:experts]

    when(ad, table)
    pl.semaphore_wait(barrier, len(greeted))

    def gather_z(i, cond):
        s = source[i]

        def body():
            if i == 0:
                for copy in own_copies():
                    copy.wait()
            else:
                n = jnp.where(s < z, 0, planes) + s
                arrive("tu", n, tabs.at[s, 0], column[i])
                arrive("ru", n, raw.at[s], column[i])

        when(cond, body)

    def pass_z(i, cond):
        s = source[i]
        go_up = cond & (s <= z) & (z < planes - 1)
        go_down = cond & (s >= z) & (z > 0)

        def up():
            send(go_up, "tu", s, lambda: (tabs.at[s, 0], tabs.at[s, 0]), above)
            send(go_up, "ru", s, lambda: (raw.at[s], raw.at[s]), above)

        def down():
            send(go_down, "td", s, lambda: (tabs.at[s, 0], tabs.at[s, 0]), below)
            send(go_down, "rd", s, lambda: (raw.at[s], raw.at[s]), below)

        when(go_up, up)
        when(go_down, down)

    def spread(i):
        s = source[i]

        def body():
            send(ad, "tx", i, lambda: (tabs.at[s, 0], tabs.at[s, 0]), to_x)
            send(ad, "ty", i, lambda: (tabs.at[s, 0], tabs.at[s, 1]), to_y)
            send(ad, "rx", i, lambda: (raw.at[s, :, :, h0], raw.at[s, :, :, h0]), to_x)
            send(ad, "ry", i, lambda: (raw.at[s, :, :, h1], raw.at[s, :, :, h1]), to_y)

        when(ad, body)

    slot = lax.broadcasted_iota(jnp.int32, (cap, rows), 0).astype(f32)

    def build(i, h, t, target):
        s = source[i]
        for n, e in ((0, target), (1, me)):
            a = jnp.where(slot == tabs[s, t, pl.ds(e, 1), :], 1.0, 0.0)
            sel[i, h, n * cap:(n + 1) * cap, :] = a.astype(bf16)
            selt[i, h, n] = a.T.astype(bf16)

    step = 256

    def pack(i, h, to_rows):
        s = source[i]
        picker = sel[i, h]

        @pl.loop(0, cut // step)
        def _(n):
            local = pl.ds(pl.multiple_of(n * step, step), step)
            cols = pl.ds(pl.multiple_of(h * cut + n * step, step), step)
            for k in range(2):
                picked = jnp.dot(picker, raw[s, k, :, cols], preferred_element_type=f32).astype(bf16)
                stage[i % 2, h, k, :, local] = picked[0:cap]
                comp[i, k, to_rows, cols] = picked[cap:]

    def settle(i):
        for h, kind in ((0, "sy"), (1, "sx")):
            staged.pop((kind, i))()

    def share(i):
        s = source[i]
        if i >= 2:
            settle(i - 2)

        def first():
            arrive("tx", i, tabs.at[s, 0], to_x)
            send(bc, "t2", i, lambda: (tabs.at[s, 0], tabs.at[s, 1]), to_y)
            arrive("rx", i, raw.at[s, :, :, h0], to_x)

        when(bc, first)
        build(i, 0, 0, peer_y)
        pack(i, 0, lo)
        send(None, "sy", i, lambda: (stage.at[i % 2, 0], comp.at[i, :, hi, h0]), to_y)

        def second():
            arrive("ty", i, tabs.at[s, 1], to_y)
            arrive("ry", i, raw.at[s, :, :, h1], to_y)

        when(bc, second)
        build(i, 1, tab1, peer_x)
        pack(i, 1, own1)
        send(None, "sx", i, lambda: (stage.at[i % 2, 1], comp.at[i, :, own1, h1]), to_x)

    def compute(i):
        s = source[i]
        arrive("sy", i, comp.at[i, :, hi, h0], to_y)
        arrive("sx", i, comp.at[i, :, other1, h1], to_x)
        when(ad, lambda: arrive("t2", i, tabs.at[s, 1], to_y))
        for k in range(2):
            hit = slot == tabs[s, k, pl.ds(me, 1), :]
            pw[k * cap:(k + 1) * cap, :] = jnp.sum(
                jnp.where(hit, tabs[s, k, pl.ds(experts + me, 1), :], 0.0), axis=1, keepdims=True)
        tile = 256

        @pl.loop(0, hidden // tile)
        def _(f):
            cols = pl.ds(pl.multiple_of(f * tile, tile), tile)
            gate = jnp.dot(comp[i, 0], wgv[:, cols], preferred_element_type=f32)
            up = jnp.dot(comp[i, 0], wuv[:, cols], preferred_element_type=f32)
            grad = lax.dot_general(comp[i, 1], wdv[cols, :], NT, preferred_element_type=f32)
            s = jax.nn.sigmoid(gate)
            gg[:, cols] = (grad * up * s * (1.0 + gate * (1.0 - s))).astype(bf16)
            ug[:, cols] = (grad * gate * s).astype(bf16)

        wide = 512

        @pl.loop(0, features // wide)
        def _(d):
            cols = pl.ds(pl.multiple_of(d * wide, wide), wide)
            back = lax.dot_general(gg[...], wgv[cols, :], NT, preferred_element_type=f32)
            back = back + lax.dot_general(ug[...], wuv[cols, :], NT, preferred_element_type=f32)
            part[i, :, cols] = (back * pw[...]).astype(bf16)

    def back1(i):
        send(None, "py", i, lambda: (part.at[i, hi, h0], rc.at[i, :, h0]), to_y)
        send(None, "px", i, lambda: (part.at[i, other1, h1], rc.at[i, :, h1]), to_x)

    def merged(i, h, n, mine):
        cols = pl.ds(pl.multiple_of(h * cut + n * step, step), step)
        value = jnp.dot(selt[i, h, 1], part[i, mine, cols], preferred_element_type=f32)
        return cols, value + jnp.dot(selt[i, h, 0], rc[i, :, cols], preferred_element_type=f32)

    def back2(i):
        def body():
            for h, kind, to, out, there, mine in (
                (0, "py", to_y, "qx", to_x, lo), (1, "px", to_x, "qy", to_y, hi)):
                half = (h0, h1)[h]
                arrive(kind, i, rc.at[i, :, half], to)

                @pl.loop(0, cut // step)
                def _(n):
                    cols, value = merged(i, h, n, mine)
                    total[i, :, cols] = value.astype(bf16)

                send(bc, out, i, lambda half=half: (total.at[i, :, half], rr.at[i, :, half]), there)

        when(bc, body)

    def back3(i):
        s = source[i]

        def body():
            if i == 0:
                for j in range(1, planes):
                    arrive("zz", source[j], r3.at[source[j]], column[j])
            for h, kind, to, out, there in ((0, "py", to_y, "qx", to_x), (1, "px", to_x, "qy", to_y)):
                half = (h0, h1)[h]
                arrive(kind, i, rc.at[i, :, half], to)
                arrive(out, i, rr.at[i, :, half], there)

                @pl.loop(0, cut // step)
                def _(n):
                    cols, value = merged(i, h, n, lo)
                    value = value + rr[i, :, cols].astype(f32)
                    if i == 0:
                        for j in range(1, planes):
                            value = value + r3[source[j], :, cols].astype(f32)
                        fin[h, :, pl.ds(pl.multiple_of(n * step, step), step)] = value.astype(bf16)
                    else:
                        total[i, :, cols] = value.astype(bf16)

            if i > 0:
                send(ad, "zz", s, lambda: (total.at[i], r3.at[z]), column[i], got=z)

        when(ad, body)

    gather_z(0, ad)
    spread(0)
    pass_z(0, ad)
    share(0)
    gather_z(1, ad)
    pass_z(1, ad)
    spread(1)
    gather_z(2, ad & inner)
    pass_z(2, ad & inner)
    share(1)
    for copy in loads:
        copy.wait()
    compute(0)
    gather_z(2, ad & outer)
    spread(2)
    gather_z(3, ad & inner)
    pass_z(3, ad & inner)
    share(2)
    compute(1)
    back1(1)
    gather_z(3, ad & outer)
    spread(3)
    back2(1)
    share(3)
    back1(0)
    compute(2)
    back1(2)
    back3(1)
    back2(2)
    compute(3)
    back1(3)
    back3(2)
    back2(3)
    back2(0)
    back3(3)
    back3(0)

    def finish():
        send(ad, "dp", 0, lambda: (fin.at[1 - core], out_ref), to_core)
        out_ref[...] = fin[core]

    when(ad, finish)
    when(bc, lambda: arrive("dp", 0, out_ref, to_core))
    for wait in staged.values():
        wait()
    for cond, wait in sent:
        if cond is None:
            wait()
        else:
            when(cond, wait)


def fused(layer_input, out_grad, expert_ids, gate_probs, gate_proj, up_proj, down_proj):
    experts, halves = lax.axis_size("ep"), lax.axis_size("dp")
    rows, features = layer_input.shape
    hidden = gate_proj.shape[2]
    planes = experts // 4
    cap = capacity(experts, expert_ids.shape)
    cut, bf16, f32 = features // 2, jnp.bfloat16, jnp.float32
    vmem, hbm = pl.BlockSpec(memory_space=pltpu.VMEM), pl.BlockSpec(memory_space=pl.ANY)
    count = 17 * planes
    return pl.pallas_call(
        functools.partial(kernel, cap),
        name="fused_backward",
        out_shape=jax.ShapeDtypeStruct((rows, cut), bf16),
        in_specs=[hbm, hbm, vmem, vmem, hbm, hbm, hbm],
        out_specs=vmem,
        scratch_shapes=[
            pltpu.VMEM((planes, 2, rows, features), bf16),
            pltpu.VMEM((planes, 2, 2 * experts, rows), f32),
            pltpu.VMEM((2, 2, 2, cap, cut), bf16),
            pltpu.VMEM((planes, 2, 2 * cap, features), bf16),
            pltpu.VMEM((planes, 2 * cap, features), bf16),
            pltpu.VMEM((planes, cap, features), bf16),
            pltpu.VMEM((planes, rows, features), bf16),
            pltpu.VMEM((planes, rows, features), bf16),
            pltpu.VMEM((planes, rows, features), bf16),
            pltpu.VMEM((planes, 2, 2 * cap, rows), bf16),
            pltpu.VMEM((planes, 2, 2, rows, cap), bf16),
            pltpu.VMEM((features, hidden), bf16),
            pltpu.VMEM((features, hidden), bf16),
            pltpu.VMEM((hidden, features), bf16),
            pltpu.VMEM((2 * cap, hidden), bf16),
            pltpu.VMEM((2 * cap, hidden), bf16),
            pltpu.VMEM((2 * cap, 1), f32),
            pltpu.VMEM((halves, rows, cut), bf16),
            pltpu.SemaphoreType.DMA((count,)),
            pltpu.SemaphoreType.DMA((count,)),
            pltpu.SemaphoreType.DMA((5,)),
        ],
        compiler_params=pltpu.CompilerParams(
            collective_id=0, has_side_effects=True, vmem_limit_bytes=67043328
        ),
    )(layer_input, out_grad, expert_ids, gate_probs, gate_proj, up_proj, down_proj)


def capacity(experts, shape):
    return 5 * shape[0] * shape[1] // (4 * experts)


def dense(layer_input, out_grad, expert_ids, gate_probs, gate_proj, up_proj, down_proj):
    experts = lax.axis_size("ep")
    halves = lax.axis_size("dp")
    tok_rows, features = layer_input.shape
    half = tok_rows // halves
    core = lax.axis_index("dp")
    start = core * half
    mine_in = lax.dynamic_slice_in_dim(layer_input, start, half, 0)
    mine_grad = lax.dynamic_slice_in_dim(out_grad, start, half, 0)
    ids = lax.dynamic_slice_in_dim(expert_ids, start, half, 0)
    probs = lax.dynamic_slice_in_dim(gate_probs, start, half, 0)
    names = jnp.arange(experts, dtype=jnp.int32)
    table = jnp.sum(
        jnp.where(ids[None, :, :] == names[:, None, None], probs[None, :, :], 0.0), axis=2
    )
    weight = lax.all_to_all(table, "ep", split_axis=0, concat_axis=0, tiled=True).reshape(-1)
    in_rows = lax.all_gather(mine_in, "ep", axis=0, tiled=True)
    grad_rows = lax.all_gather(mine_grad, "ep", axis=0, tiled=True)
    gate_mat, up_mat, down_mat = (gate_proj[0], up_proj[0], down_proj[0])
    nt = (((1,), (1,)), ((), ()))
    gate_pre = jnp.dot(in_rows, gate_mat, preferred_element_type=jnp.float32)
    up_pre = jnp.dot(in_rows, up_mat, preferred_element_type=jnp.float32)
    hidden_grad = lax.dot_general(grad_rows, down_mat, nt, preferred_element_type=jnp.float32)
    s = jax.nn.sigmoid(gate_pre)
    gate_grad = (hidden_grad * up_pre * s * (1.0 + gate_pre * (1.0 - s))).astype(jnp.bfloat16)
    up_grad = (hidden_grad * gate_pre * s).astype(jnp.bfloat16)
    back = lax.dot_general(gate_grad, gate_mat, nt, preferred_element_type=jnp.float32)
    back = back + lax.dot_general(up_grad, up_mat, nt, preferred_element_type=jnp.float32)
    back = (back * weight[:, None]).astype(jnp.bfloat16)
    mine = lax.psum_scatter(back, "ep", scatter_dimension=0, tiled=True)
    return lax.all_to_all(mine, "dp", split_axis=1, concat_axis=0, tiled=True)


def body(*args):
    experts, halves = lax.axis_size("ep"), lax.axis_size("dp")
    rows, features = args[0].shape
    hidden = args[4].shape[2]
    cap = capacity(experts, args[2].shape)
    planes = experts // 4
    held = 2 * features * (planes * (5 * rows + 7 * cap) + 3 * hidden + rows + 8 * cap)
    fits = held < 64 * 10**6 and halves == 2 and experts == 16 and cap % 16 == 0
    return (fused if fits else dense)(*args)


def solution(mesh):
    row = P("ep", None)
    mat = P("ep", None, None)
    return jax.shard_map(
        body, mesh=mesh, in_specs=(row, row, row, row, mat, mat, mat), out_specs=P("ep", "dp"), check_vma=False
    )
```

time: 233 us -> 188 us (0.81)
  the two profiles are of different devices: /device:TPU:17 before, /device:TPU:0 now
where the time goes in v1:
time: 188 us
  Pallas kernels  183 us (97%)
  local copies, waits for them, and re-layouts  4.63 us (2%)
    pallas_call x1, Pallas kernels, fused(): pl.pallas_call(functools.partial(kernel, cap), name='fused_backward', out...  183 us
    unnamed x3, local copies, waits for them, and re-layouts  4.63 us

profile of v1, /device:TPU:0, one launch (start us, length us, event | category | flops | bytes accessed | tf_op | source)
XLA Modules:
  0.0 187.6 jit_solution(3210091500582025678)
XLA Ops:
  0.0 1.4 copy.8.ids_ref
  1.4 1.4 copy.9.prob_ref
  2.8 182.9 %fused_backward.1 = bf16[128,1792]{1,0:T(8,128)(2,1)} custom-call(bf16[128,3584]{1,0:T(8,128)(2,1)} %x_hbm.1, bf16[128,3584]{1,0:T(8,128)(2,1)} %g_hbm.1, s32[128,8]{1,0:T(8,128)} %copy.8.ids_ref, f32[128,8]{1,0:T(8,128)} %copy.9.prob_ref, bf16[1,3584,1024]{2,1,0:T(8,128)(2,1)} %wg_hbm.1, bf16[1,3584,1024]{2,1,0:T(8,128)(2,1)} %wu_hbm.1, ...), custom_call_target="tpu_custom_call" | custom-call | tf_op jit(solution)/shard_map/fused_backward/pallas_call | solution.py:349
  185.8 1.8 copy.11

commit v2 on v1

--- a/solution.py
+++ b/solution.py
@@ -11,8 +11,19 @@
 NT = (((1,), (1,)), ((), ()))
 
 
-def kernel(cap, x_hbm, g_hbm, ids_ref, prob_ref, wg_hbm, wu_hbm, wd_hbm, out_ref,
-           raw, tabs, stage, comp, part, rc, rr, total, r3, sel, selt, wgv, wuv, wdv, gg, ug, pw, fin,
+STEPS = (
+    ("gz", 0), ("sp", 0), ("sy", 0), ("sx", 0), ("gz", 1), ("sp", 1), ("go", 2), ("gi", 2),
+    ("sp", 2), ("sy", 1), ("sx", 1), ("sx", 2), ("sy", 2), ("go", 3), ("gi", 3), ("cf", 1),
+    ("sp", 3), ("cf", 2), ("sx", 3), ("cb", 2), ("sy", 3), ("ca", 2), ("cb", 1), ("cf", 0),
+    ("1x", 2), ("2x", 2), ("ca", 1), ("1x", 1), ("2x", 1), ("1y", 2), ("2y", 2), ("1y", 1),
+    ("cf", 3), ("cb", 3), ("2y", 1), ("3x", 2), ("ca", 3), ("1x", 3), ("cb", 0), ("3y", 2),
+    ("3x", 1), ("2x", 3), ("1y", 3), ("ca", 0), ("3y", 1), ("3x", 3), ("2y", 3), ("1x", 0),
+    ("3y", 3), ("1y", 0), ("2x", 0), ("2y", 0), ("3x", 0), ("3y", 0),
+)
+
+
+def kernel(cap, x_hbm, g_hbm, ids_hbm, prob_hbm, wg_hbm, wu_hbm, wd_hbm, out_ref,
+           raw, tabs, stage, comp, part, rc, rr, total, r3, sel, selt, wgv, wuv, wdv, gg, ug, pw, fin, ids_ref, prob_ref,
            send_sem, recv_sem, load_sem):
     me, core = lax.axis_index("ep"), lax.axis_index("dp")
     z, y, x = me // 4, (me // 2) % 2, me % 2
@@ -38,7 +49,7 @@
     own1 = pl.ds(pl.multiple_of(off1, 16), cap)
     other1 = pl.ds(pl.multiple_of(cap - off1, 16), cap)
 
-    kinds = ("ru", "rd", "tu", "td", "rx", "ry", "tx", "ty", "t2", "sx", "sy", "px", "py", "qx", "qy", "zz", "dp")
+    kinds = ("ru", "rd", "tu", "td", "rx", "ry", "tx", "ty", "t2", "sx", "sy", "px", "py", "qx", "qy", "z0", "z1", "dp")
     sent, staged = [], {}
 
     def number(kind, i):
@@ -71,6 +82,12 @@
         pltpu.make_async_copy(wd_hbm.at[0], wdv, load_sem.at[4]),
     ]
 
+    def own_lists():
+        return [
+            pltpu.make_async_copy(ids_hbm, ids_ref, load_sem.at[5]),
+            pltpu.make_async_copy(prob_hbm, prob_ref, load_sem.at[6]),
+        ]
+
     def own_copies():
         return [
             pltpu.make_async_copy(x_hbm, raw.at[z, 0], load_sem.at[0]),
@@ -78,7 +95,7 @@
         ]
 
     def begin():
-        for copy in own_copies():
+        for copy in own_lists() + own_copies():
             copy.start()
 
     when(ad, begin)
@@ -92,6 +109,8 @@
         pl.semaphore_signal(barrier, inc=1, device_id=other, device_id_type=MESH)
 
     def table():
+        for copy in own_lists():
+            copy.wait()
         name = lax.broadcasted_iota(jnp.int32, (rows, 128), 1)
         count = jnp.zeros((rows, 128), f32)
         prob = jnp.zeros((rows, 128), f32)
@@ -159,7 +178,7 @@
             sel[i, h, n * cap:(n + 1) * cap, :] = a.astype(bf16)
             selt[i, h, n] = a.T.astype(bf16)
 
-    step = 256
+    step = cut // 2 if cut % 256 == 0 else cut
 
     def pack(i, h, to_rows):
         s = source[i]
@@ -167,21 +186,17 @@
 
         @pl.loop(0, cut // step)
         def _(n):
-            local = pl.ds(pl.multiple_of(n * step, step), step)
-            cols = pl.ds(pl.multiple_of(h * cut + n * step, step), step)
+            local = pl.ds(pl.multiple_of(n * step, 128), step)
+            cols = pl.ds(pl.multiple_of(h * cut + n * step, 128), step)
             for k in range(2):
                 picked = jnp.dot(picker, raw[s, k, :, cols], preferred_element_type=f32).astype(bf16)
                 stage[i % 2, h, k, :, local] = picked[0:cap]
                 comp[i, k, to_rows, cols] = picked[cap:]
 
-    def settle(i):
-        for h, kind in ((0, "sy"), (1, "sx")):
-            staged.pop((kind, i))()
-
-    def share(i):
+    def share_y(i):
         s = source[i]
         if i >= 2:
-            settle(i - 2)
+            staged.pop(("sy", i - 2))()
 
         def first():
             arrive("tx", i, tabs.at[s, 0], to_x)
@@ -193,6 +208,11 @@
         pack(i, 0, lo)
         send(None, "sy", i, lambda: (stage.at[i % 2, 0], comp.at[i, :, hi, h0]), to_y)
 
+    def share_x(i):
+        s = source[i]
+        if i >= 2:
+            staged.pop(("sx", i - 2))()
+
         def second():
             arrive("ty", i, tabs.at[s, 1], to_y)
             arrive("ry", i, raw.at[s, :, :, h1], to_y)
@@ -202,14 +222,14 @@
         pack(i, 1, own1)
         send(None, "sx", i, lambda: (stage.at[i % 2, 1], comp.at[i, :, own1, h1]), to_x)
 
-    def compute(i):
+    def forward(i):
         s = source[i]
         arrive("sy", i, comp.at[i, :, hi, h0], to_y)
         arrive("sx", i, comp.at[i, :, other1, h1], to_x)
         when(ad, lambda: arrive("t2", i, tabs.at[s, 1], to_y))
         for k in range(2):
             hit = slot == tabs[s, k, pl.ds(me, 1), :]
-            pw[k * cap:(k + 1) * cap, :] = jnp.sum(
+            pw[i, k * cap:(k + 1) * cap, :] = jnp.sum(
                 jnp.where(hit, tabs[s, k, pl.ds(experts + me, 1), :], 0.0), axis=1, keepdims=True)
         tile = 256
 
@@ -220,114 +240,98 @@
             up = jnp.dot(comp[i, 0], wuv[:, cols], preferred_element_type=f32)
             grad = lax.dot_general(comp[i, 1], wdv[cols, :], NT, preferred_element_type=f32)
             s = jax.nn.sigmoid(gate)
-            gg[:, cols] = (grad * up * s * (1.0 + gate * (1.0 - s))).astype(bf16)
-            ug[:, cols] = (grad * gate * s).astype(bf16)
-
-        wide = 512
-
-        @pl.loop(0, features // wide)
+            gg[i, :, cols] = (grad * up * s * (1.0 + gate * (1.0 - s))).astype(bf16)
+            ug[i, :, cols] = (grad * gate * s).astype(bf16)
+
+    def backward(i, h):
+        @pl.loop(0, cut // step)
         def _(d):
-            cols = pl.ds(pl.multiple_of(d * wide, wide), wide)
-            back = lax.dot_general(gg[...], wgv[cols, :], NT, preferred_element_type=f32)
-            back = back + lax.dot_general(ug[...], wuv[cols, :], NT, preferred_element_type=f32)
-            part[i, :, cols] = (back * pw[...]).astype(bf16)
-
-    def back1(i):
+            cols = pl.ds(pl.multiple_of(h * cut + d * step, 128), step)
+            back = lax.dot_general(gg[i], wgv[cols, :], NT, preferred_element_type=f32)
+            back = back + lax.dot_general(ug[i], wuv[cols, :], NT, preferred_element_type=f32)
+            part[i, :, cols] = (back * pw[i]).astype(bf16)
+
+    def back1_y(i):
         send(None, "py", i, lambda: (part.at[i, hi, h0], rc.at[i, :, h0]), to_y)
+
+    def back1_x(i):
         send(None, "px", i, lambda: (part.at[i, other1, h1], rc.at[i, :, h1]), to_x)
 
     def merged(i, h, n, mine):
-        cols = pl.ds(pl.multiple_of(h * cut + n * step, step), step)
+        cols = pl.ds(pl.multiple_of(h * cut + n * step, 128), step)
         value = jnp.dot(selt[i, h, 1], part[i, mine, cols], preferred_element_type=f32)
         return cols, value + jnp.dot(selt[i, h, 0], rc[i, :, cols], preferred_element_type=f32)
 
-    def back2(i):
+    routes = (("py", to_y, "qx", to_x, h0, lo), ("px", to_x, "qy", to_y, h1, hi))
+
+    def back2(i, h):
+        kind, to, out, there, half, mine = routes[h]
+
         def body():
-            for h, kind, to, out, there, mine in (
-                (0, "py", to_y, "qx", to_x, lo), (1, "px", to_x, "qy", to_y, hi)):
-                half = (h0, h1)[h]
-                arrive(kind, i, rc.at[i, :, half], to)
-
-                @pl.loop(0, cut // step)
-                def _(n):
-                    cols, value = merged(i, h, n, mine)
-                    total[i, :, cols] = value.astype(bf16)
-
-                send(bc, out, i, lambda half=half: (total.at[i, :, half], rr.at[i, :, half]), there)
+            arrive(kind, i, rc.at[i, :, half], to)
+
+            @pl.loop(0, cut // step)
+            def _(n):
+                cols, value = merged(i, h, n, mine)
+                total[i, :, cols] = value.astype(bf16)
+
+            send(bc, out, i, lambda: (total.at[i, :, half], rr.at[i, :, half]), there)
 
         when(bc, body)
 
-    def back3(i):
-        s = source[i]
+    def back3(i, h):
+        s = source[i]
+        kind, to, out, there, half, mine = routes[h]
+        home = ("z0", "z1")[h]
 
         def body():
+            arrive(kind, i, rc.at[i, :, half], to)
+            arrive(out, i, rr.at[i, :, half], there)
             if i == 0:
                 for j in range(1, planes):
-                    arrive("zz", source[j], r3.at[source[j]], column[j])
-            for h, kind, to, out, there in ((0, "py", to_y, "qx", to_x), (1, "px", to_x, "qy", to_y)):
-                half = (h0, h1)[h]
-                arrive(kind, i, rc.at[i, :, half], to)
-                arrive(out, i, rr.at[i, :, half], there)
-
-                @pl.loop(0, cut // step)
-                def _(n):
-                    cols, value = merged(i, h, n, lo)
-                    value = value + rr[i, :, cols].astype(f32)
-                    if i == 0:
-                        for j in range(1, planes):
-                            value = value + r3[source[j], :, cols].astype(f32)
-                        fin[h, :, pl.ds(pl.multiple_of(n * step, step), step)] = value.astype(bf16)
-                    else:
-                        total[i, :, cols] = value.astype(bf16)
+                    arrive(home, source[j], r3.at[source[j], :, half], column[j])
+
+            @pl.loop(0, cut // step)
+            def _(n):
+                cols, value = merged(i, h, n, lo)
+                value = value + rr[i, :, cols].astype(f32)
+                if i == 0:
+                    for j in range(1, planes):
+                        value = value + r3[source[j], :, cols].astype(f32)
+                    fin[h, :, pl.ds(pl.multiple_of(n * step, 128), step)] = value.astype(bf16)
+                else:
+                    total[i, :, cols] = value.astype(bf16)
 
             if i > 0:
-                send(ad, "zz", s, lambda: (total.at[i], r3.at[z]), column[i], got=z)
+                send(ad, home, s, lambda: (total.at[i, :, half], r3.at[z, :, half]), column[i], got=z)
 
         when(ad, body)
-
-    gather_z(0, ad)
-    spread(0)
-    pass_z(0, ad)
-    share(0)
-    gather_z(1, ad)
-    pass_z(1, ad)
-    spread(1)
-    gather_z(2, ad & inner)
-    pass_z(2, ad & inner)
-    share(1)
-    for copy in loads:
-        copy.wait()
-    compute(0)
-    gather_z(2, ad & outer)
-    spread(2)
-    gather_z(3, ad & inner)
-    pass_z(3, ad & inner)
-    share(2)
-    compute(1)
-    back1(1)
-    gather_z(3, ad & outer)
-    spread(3)
-    back2(1)
-    share(3)
-    back1(0)
-    compute(2)
-    back1(2)
-    back3(1)
-    back2(2)
-    compute(3)
-    back1(3)
-    back3(2)
-    back2(3)
-    back2(0)
-    back3(3)
-    back3(0)
+        if i == 0:
+            over = ad & (core != h)
+            when(over, lambda: send(over, "dp", h, lambda: (fin.at[h], out_ref), to_core))
+
+    ops = {
+        "sp": spread,
+        "gz": lambda i: (gather_z(i, ad), pass_z(i, ad)),
+        "gi": lambda i: (gather_z(i, ad & inner), pass_z(i, ad & inner)),
+        "go": lambda i: gather_z(i, ad & outer),
+        "sy": share_y, "sx": share_x, "cf": forward,
+        "ca": lambda i: backward(i, 0), "cb": lambda i: backward(i, 1),
+        "1y": back1_y, "1x": back1_x,
+        "2y": lambda i: back2(i, 0), "2x": lambda i: back2(i, 1),
+        "3y": lambda i: back3(i, 0), "3x": lambda i: back3(i, 1),
+    }
+    for name, i in STEPS:
+        if name == "cf":
+            while loads:
+                loads.pop().wait()
+        ops[name](i)
 
     def finish():
-        send(ad, "dp", 0, lambda: (fin.at[1 - core], out_ref), to_core)
         out_ref[...] = fin[core]
 
     when(ad, finish)
-    when(bc, lambda: arrive("dp", 0, out_ref, to_core))
+    when(bc, lambda: arrive("dp", core, out_ref, to_core))
     for wait in staged.values():
         wait()
     for cond, wait in sent:
@@ -345,12 +349,12 @@
     cap = capacity(experts, expert_ids.shape)
     cut, bf16, f32 = features // 2, jnp.bfloat16, jnp.float32
     vmem, hbm = pl.BlockSpec(memory_space=pltpu.VMEM), pl.BlockSpec(memory_space=pl.ANY)
-    count = 17 * planes
+    count = 18 * planes
     return pl.pallas_call(
         functools.partial(kernel, cap),
         name="fused_backward",
         out_shape=jax.ShapeDtypeStruct((rows, cut), bf16),
-        in_specs=[hbm, hbm, vmem, vmem, hbm, hbm, hbm],
+        in_specs=[hbm] * 7,
         out_specs=vmem,
         scratch_shapes=[
             pltpu.VMEM((planes, 2, rows, features), bf16),
@@ -367,13 +371,15 @@
             pltpu.VMEM((features, hidden), bf16),
             pltpu.VMEM((features, hidden), bf16),
             pltpu.VMEM((hidden, features), bf16),
-            pltpu.VMEM((2 * cap, hidden), bf16),
-            pltpu.VMEM((2 * cap, hidden), bf16),
-            pltpu.VMEM((2 * cap, 1), f32),
+            pltpu.VMEM((planes, 2 * cap, hidden), bf16),
+            pltpu.VMEM((planes, 2 * cap, hidden), bf16),
+            pltpu.VMEM((planes, 2 * cap, 1), f32),
             pltpu.VMEM((halves, rows, cut), bf16),
+            pltpu.VMEM(expert_ids.shape, jnp.int32),
+            pltpu.VMEM(gate_probs.shape, f32),
             pltpu.SemaphoreType.DMA((count,)),
             pltpu.SemaphoreType.DMA((count,)),
-            pltpu.SemaphoreType.DMA((5,)),
+            pltpu.SemaphoreType.DMA((7,)),
         ],
         compiler_params=pltpu.CompilerParams(
             collective_id=0, has_side_effects=True, vmem_limit_bytes=67043328

time: 188 us -> 169 us (0.90)
  Pallas kernels: 183 us -> 162 us
    pallas_call x1, Pallas kernels: 183 us -> 162 us  [fused(): pl.pallas_call(functools.partial(kernel, cap), name='fused_backward', out...]
where the time goes in v2:
time: 169 us; the launch traced here: 167 us
  Pallas kernels  162 us (96%)
  local copies, waits for them, and re-layouts  4.63 us (3%)
    pallas_call x1, Pallas kernels, fused(): pl.pallas_call(functools.partial(kernel, cap), name='fused_backward', out...  162 us
    unnamed x3, local copies, waits for them, and re-layouts  4.63 us

profile of v2, /device:TPU:0, one launch (start us, length us, event | category | flops | bytes accessed | tf_op | source)
XLA Modules:
  0.0 167.1 jit_solution(14065347185385414261)
XLA Ops:
  0.0 1.4 copy.8.ids_hbm
  1.4 1.4 copy.9.prob_hbm
  2.8 162.5 %fused_backward.1 = bf16[128,1792]{1,0:T(8,128)(2,1)} custom-call(bf16[128,3584]{1,0:T(8,128)(2,1)} %x_hbm.1, bf16[128,3584]{1,0:T(8,128)(2,1)} %g_hbm.1, s32[128,8]{1,0:T(8,128)} %copy.8.ids_hbm, f32[128,8]{1,0:T(8,128)} %copy.9.prob_hbm, bf16[1,3584,1024]{2,1,0:T(8,128)(2,1)} %wg_hbm.1, bf16[1,3584,1024]{2,1,0:T(8,128)(2,1)} %wu_hbm.1, ...), custom_call_target="tpu_custom_call" | custom-call | tf_op jit(solution)/shard_map/fused_backward/pallas_call | solution.py:353
  165.3 1.8 %copy.11 = bf16[128,1792]{1,0:T(8,128)(2,1)} copy(bf16[128,1792]{1,0:T(8,128)(2,1)} %fused_backward.1) | data formatting | bytes 917504

commit v3 on v2

--- a/solution.py
+++ b/solution.py
@@ -11,23 +11,26 @@
 NT = (((1,), (1,)), ((), ()))
 
 
+LINE = 4
+
 STEPS = (
-    ("gz", 0), ("sp", 0), ("sy", 0), ("sx", 0), ("gz", 1), ("sp", 1), ("go", 2), ("gi", 2),
-    ("sp", 2), ("sy", 1), ("sx", 1), ("sx", 2), ("sy", 2), ("go", 3), ("gi", 3), ("cf", 1),
-    ("sp", 3), ("cf", 2), ("sx", 3), ("cb", 2), ("sy", 3), ("ca", 2), ("cb", 1), ("cf", 0),
-    ("1x", 2), ("2x", 2), ("ca", 1), ("1x", 1), ("2x", 1), ("1y", 2), ("2y", 2), ("1y", 1),
-    ("cf", 3), ("cb", 3), ("2y", 1), ("3x", 2), ("ca", 3), ("1x", 3), ("cb", 0), ("3y", 2),
-    ("3x", 1), ("2x", 3), ("1y", 3), ("ca", 0), ("3y", 1), ("3x", 3), ("2y", 3), ("1x", 0),
-    ("3y", 3), ("1y", 0), ("2x", 0), ("2y", 0), ("3x", 0), ("3y", 0),
+    ("gz", 0), ("sp", 0), ("v0", 0), ("tb", 0), ("v1", 0), ("sx", 0), ("sy", 0), ("gz", 1), ("gi", 2),
+    ("sp", 1), ("sx", 1), ("za", 0), ("sy", 1), ("zb", 0), ("cf", 0), ("go", 2), ("cb", 0),
+    ("sp", 2), ("gi", 3), ("ra", 1), ("rb", 1), ("sx", 2), ("sy", 2), ("cf", 1), ("ca", 1),
+    ("cb", 1), ("go", 3), ("sp", 3), ("ra", 2), ("rb", 2), ("sy", 3), ("sx", 3), ("cf", 2),
+    ("1x", 1), ("ca", 2), ("1y", 2), ("1y", 1), ("cb", 2), ("2y", 2), ("1x", 2), ("ca", 0),
+    ("2x", 2), ("rb", 3), ("2x", 1), ("2y", 1), ("ra", 3), ("cf", 3), ("3y", 2), ("cb", 3),
+    ("ca", 3), ("3x", 2), ("1x", 3), ("2x", 3), ("1y", 3), ("2y", 3), ("1x", 0), ("2x", 0),
+    ("3x", 1), ("1y", 0), ("3y", 1), ("2y", 0), ("3x", 3), ("3y", 3), ("3x", 0), ("3y", 0),
 )
 
 
 def kernel(cap, x_hbm, g_hbm, ids_hbm, prob_hbm, wg_hbm, wu_hbm, wd_hbm, out_ref,
-           raw, tabs, stage, comp, part, rc, rr, total, r3, sel, selt, wgv, wuv, wdv, gg, ug, pw, fin, ids_ref, prob_ref,
+           raw, rawv, tabs, stage, stagev, comp, part, rc, rr, r3, sel, selt, wgv, wuv, wdv, gg, ug, pw, ids_ref, prob_ref,
            send_sem, recv_sem, load_sem):
     me, core = lax.axis_index("ep"), lax.axis_index("dp")
     z, y, x = me // 4, (me // 2) % 2, me % 2
-    planes, rows, features = raw.shape[0], raw.shape[2], raw.shape[3]
+    planes, rows, features = comp.shape[0], raw.shape[2], comp.shape[3]
     hidden, experts = wgv.shape[1], tabs.shape[2] // 2
     cut = features // 2
     f32, bf16 = jnp.float32, jnp.bfloat16
@@ -44,12 +47,19 @@
     column = [{"ep": s * 4 + y * 2 + x} for s in source]
     above = {"ep": jnp.minimum(z + 1, planes - 1) * 4 + y * 2 + x}
     below = {"ep": jnp.maximum(z - 1, 0) * 4 + y * 2 + x}
+    near, aside = raw.shape[3] // 2, rawv.shape[4]
+    a0, a1, av = pl.ds(0, near), pl.ds(near, near), pl.ds(2 * near, aside)
     h0, h1 = pl.ds(0, cut), pl.ds(cut, cut)
+    slots = (pl.ds(0, cap), pl.ds(cap, cap))
+    end = (planes - 1) * far * 4 + y * 2 + x
+    toward = {"ep": jnp.where(inner, 2 - far, 1 + far) * 4 + y * 2 + x}
+    to_end = {"ep": end}
     lo, hi = pl.ds(0, cap), pl.ds(cap, cap)
     own1 = pl.ds(pl.multiple_of(off1, 16), cap)
     other1 = pl.ds(pl.multiple_of(cap - off1, 16), cap)
 
-    kinds = ("ru", "rd", "tu", "td", "rx", "ry", "tx", "ty", "t2", "sx", "sy", "px", "py", "qx", "qy", "z0", "z1", "dp")
+    kinds = ("ru", "rd", "tu", "td", "rx", "ry", "tx", "ty", "t2", "sx", "sy", "px", "py", "qx", "qy", "z0", "z1", "dp",
+             "va", "vb", "ea", "eb", "vx", "vy", "wx", "wy")
     sent, staged = [], {}
 
     def number(kind, i):
@@ -90,8 +100,10 @@
 
     def own_copies():
         return [
-            pltpu.make_async_copy(x_hbm, raw.at[z, 0], load_sem.at[0]),
-            pltpu.make_async_copy(g_hbm, raw.at[z, 1], load_sem.at[1]),
+            pltpu.make_async_copy(x_hbm.at[:, pl.ds(0, 2 * near)], raw.at[z, 0], load_sem.at[0]),
+            pltpu.make_async_copy(g_hbm.at[:, pl.ds(0, 2 * near)], raw.at[z, 1], load_sem.at[1]),
+            pltpu.make_async_copy(x_hbm.at[:, av], rawv.at[z, 0, 0], load_sem.at[7]),
+            pltpu.make_async_copy(g_hbm.at[:, av], rawv.at[z, 0, 1], load_sem.at[8]),
         ]
 
     def begin():
@@ -125,48 +137,62 @@
         tabs[z, 0, 0:experts, :] = code.T[0:experts]
         tabs[z, 0, experts:, :] = prob.T[0:experts]
 
-    when(ad, table)
+    def ready():
+        for copy in own_copies():
+            copy.wait()
+
     pl.semaphore_wait(barrier, len(greeted))
+    when(ad, ready)
 
     def gather_z(i, cond):
         s = source[i]
 
         def body():
-            if i == 0:
-                for copy in own_copies():
-                    copy.wait()
-            else:
-                n = jnp.where(s < z, 0, planes) + s
-                arrive("tu", n, tabs.at[s, 0], column[i])
-                arrive("ru", n, raw.at[s], column[i])
-
-        when(cond, body)
-
-    def pass_z(i, cond):
+            n = jnp.where(s < z, 0, planes) + s
+            arrive("tu", n, tabs.at[s, 0], column[i])
+            arrive("ru", n, raw.at[s], column[i])
+
+        if i > 0:
+            when(cond, body)
+
+    def pass_z(i, cond, names="tr"):
         s = source[i]
         go_up = cond & (s <= z) & (z < planes - 1)
         go_down = cond & (s >= z) & (z > 0)
 
-        def up():
-            send(go_up, "tu", s, lambda: (tabs.at[s, 0], tabs.at[s, 0]), above)
-            send(go_up, "ru", s, lambda: (raw.at[s], raw.at[s]), above)
-
-        def down():
-            send(go_down, "td", s, lambda: (tabs.at[s, 0], tabs.at[s, 0]), below)
-            send(go_down, "rd", s, lambda: (raw.at[s], raw.at[s]), below)
-
-        when(go_up, up)
-        when(go_down, down)
-
-    def spread(i):
+        def up(names):
+            if "t" in names:
+                send(go_up, "tu", s, lambda: (tabs.at[s, 0], tabs.at[s, 0]), above)
+            if "r" in names:
+                send(go_up, "ru", s, lambda: (raw.at[s], raw.at[s]), above)
+
+        def down(names):
+            if "t" in names:
+                send(go_down, "td", s, lambda: (tabs.at[s, 0], tabs.at[s, 0]), below)
+            if "r" in names:
+                send(go_down, "rd", s, lambda: (raw.at[s], raw.at[s]), below)
+
+        when(go_up, lambda: up(names))
+        when(go_down, lambda: down(names))
+
+    def spread_table(i):
         s = source[i]
 
         def body():
             send(ad, "tx", i, lambda: (tabs.at[s, 0], tabs.at[s, 0]), to_x)
             send(ad, "ty", i, lambda: (tabs.at[s, 0], tabs.at[s, 1]), to_y)
-            send(ad, "rx", i, lambda: (raw.at[s, :, :, h0], raw.at[s, :, :, h0]), to_x)
-            send(ad, "ry", i, lambda: (raw.at[s, :, :, h1], raw.at[s, :, :, h1]), to_y)
-
+
+        when(ad, body)
+
+    def spread(i):
+        s = source[i]
+
+        def body():
+            send(ad, "rx", i, lambda: (raw.at[s, :, :, a0], raw.at[s, :, :, a0]), to_x)
+            send(ad, "ry", i, lambda: (raw.at[s, :, :, a1], raw.at[s, :, :, a1]), to_y)
+
+        if i > 0:
+            spread_table(i)
         when(ad, body)
 
     slot = lax.broadcasted_iota(jnp.int32, (cap, rows), 0).astype(f32)
@@ -184,15 +210,94 @@
         s = source[i]
         picker = sel[i, h]
 
-        @pl.loop(0, cut // step)
+        span = near // 2 if near % 256 == 0 else near
+
+        @pl.loop(0, near // span)
         def _(n):
-            local = pl.ds(pl.multiple_of(n * step, 128), step)
-            cols = pl.ds(pl.multiple_of(h * cut + n * step, 128), step)
+            local = pl.ds(pl.multiple_of(n * span, 128), span)
+            cols = pl.ds(pl.multiple_of(h * near + n * span, 128), span)
             for k in range(2):
                 picked = jnp.dot(picker, raw[s, k, :, cols], preferred_element_type=f32).astype(bf16)
                 stage[i % 2, h, k, :, local] = picked[0:cap]
                 comp[i, k, to_rows, cols] = picked[cap:]
 
+    def plane_out(i):
+        def body():
+            send(ad, "vx", i, lambda: (rawv.at[z, 0], rawv.at[z, 0]), to_x)
+            send(ad, "vy", i, lambda: (rawv.at[z, 0], rawv.at[z, 1]), to_y)
+
+        when(ad, body)
+
+    def plane_on(i):
+        def left(k):
+            return rawv.at[z, k, :, :, pl.ds(0, aside // 2)]
+
+        def right(k):
+            return rawv.at[z, k, :, :, pl.ds(aside // 2, aside // 2)]
+
+        def body():
+            arrive("vx", i, rawv.at[z, 0], to_x)
+            send(bc, "wy", i, lambda: (left(0), left(1)), to_y)
+            arrive("vy", i, rawv.at[z, 1], to_y)
+            send(bc, "wx", i, lambda: (right(1), right(1)), to_x)
+
+        when(bc, body)
+
+    def diagonal_in(i):
+        def body():
+            arrive("wy", i, rawv.at[z, 1, :, :, pl.ds(0, aside // 2)], to_y)
+            arrive("wx", i, rawv.at[z, 1, :, :, pl.ds(aside // 2, aside // 2)], to_x)
+            arrive("t2", i, tabs.at[z, 1], to_y)
+
+        when(ad, body)
+
+    def pass_v(i, k):
+        s = source[i]
+        kind, kept = ("va", "vb")[k], ("ea", "eb")[k]
+        place = {0: 0, 2: 1, 3: 2}.get(i)
+
+        def on():
+            got = jnp.where(outer, 1, 2) if i == 0 else 3
+            make(kind, i, rawv.at[s, k], rawv.at[s, k], toward, got).start()
+
+        def on_done():
+            make(kind, i, rawv.at[s, k], rawv.at[s, k], toward, 0).wait_send()
+
+        if i == 0:
+            on()
+            sent.append((None, on_done))
+        elif i == 1:
+            on()
+            sent.append((inner, on_done))
+        mine = jnp.where(slot == tabs[s, k, pl.ds(me, 1), :], 1.0, 0.0).astype(bf16)
+        picker = mine
+        if place is not None:
+            theirs = jnp.where(slot == tabs[s, k, pl.ds(end, 1), :], 1.0, 0.0).astype(bf16)
+            picker = jnp.concatenate([mine, theirs], axis=0)
+        for n in range(2):
+            picked = jnp.dot(picker, rawv[s, k, n], preferred_element_type=f32).astype(bf16)
+            comp[i, n, slots[k], av] = picked[0:cap]
+            if place is not None:
+                stagev[place, k, n] = picked[cap:]
+
+        def out():
+            there = max(i, 1)
+            send(inner, kept, i, lambda: (stagev.at[place, k], comp.at[there, :, slots[k], av]), to_end, got=there)
+
+        if place is not None:
+            when(inner, out)
+
+    def relay_v(i, k):
+        s = source[i]
+
+        def body():
+            arrive(("va", "vb")[k], i, rawv.at[s, k], toward)
+            if k == 1:
+                when(ad, lambda: arrive("t2", i, tabs.at[s, 1], to_y))
+            pass_v(i, k)
+
+        when(inner, body)
+
     def share_y(i):
         s = source[i]
         if i >= 2:
@@ -201,12 +306,12 @@
         def first():
             arrive("tx", i, tabs.at[s, 0], to_x)
             send(bc, "t2", i, lambda: (tabs.at[s, 0], tabs.at[s, 1]), to_y)
-            arrive("rx", i, raw.at[s, :, :, h0], to_x)
+            arrive("rx", i, raw.at[s, :, :, a0], to_x)
 
         when(bc, first)
         build(i, 0, 0, peer_y)
         pack(i, 0, lo)
-        send(None, "sy", i, lambda: (stage.at[i % 2, 0], comp.at[i, :, hi, h0]), to_y)
+        send(None, "sy", i, lambda: (stage.at[i % 2, 0], comp.at[i, :, hi, a0]), to_y)
 
     def share_x(i):
         s = source[i]
@@ -215,18 +320,21 @@
 
         def second():
             arrive("ty", i, tabs.at[s, 1], to_y)
-            arrive("ry", i, raw.at[s, :, :, h1], to_y)
+            arrive("ry", i, raw.at[s, :, :, a1], to_y)
 
         when(bc, second)
         build(i, 1, tab1, peer_x)
         pack(i, 1, own1)
-        send(None, "sx", i, lambda: (stage.at[i % 2, 1], comp.at[i, :, own1, h1]), to_x)
+        send(None, "sx", i, lambda: (stage.at[i % 2, 1], comp.at[i, :, own1, a1]), to_x)
 
     def forward(i):
         s = source[i]
-        arrive("sy", i, comp.at[i, :, hi, h0], to_y)
-        arrive("sx", i, comp.at[i, :, other1, h1], to_x)
-        when(ad, lambda: arrive("t2", i, tabs.at[s, 1], to_y))
+        arrive("sy", i, comp.at[i, :, hi, a0], to_y)
+        arrive("sx", i, comp.at[i, :, other1, a1], to_x)
+        if i > 0:
+            when(ad & outer, lambda: arrive("t2", i, tabs.at[s, 1], to_y))
+            for k in range(2):
+                when(outer, lambda k=k: arrive(("ea", "eb")[k], i, comp.at[i, :, slots[k], av], to_end))
         for k in range(2):
             hit = slot == tabs[s, k, pl.ds(me, 1), :]
             pw[i, k * cap:(k + 1) * cap, :] = jnp.sum(
@@ -273,9 +381,9 @@
             @pl.loop(0, cut // step)
             def _(n):
                 cols, value = merged(i, h, n, mine)
-                total[i, :, cols] = value.astype(bf16)
-
-            send(bc, out, i, lambda: (total.at[i, :, half], rr.at[i, :, half]), there)
+                rr[i, :, cols] = value.astype(bf16)
+
+            send(bc, out, i, lambda: (rr.at[i, :, half], rr.at[i, :, half]), there)
 
         when(bc, body)
 
@@ -298,23 +406,25 @@
                 if i == 0:
                     for j in range(1, planes):
                         value = value + r3[source[j], :, cols].astype(f32)
-                    fin[h, :, pl.ds(pl.multiple_of(n * step, 128), step)] = value.astype(bf16)
-                else:
-                    total[i, :, cols] = value.astype(bf16)
+                rr[i, :, cols] = value.astype(bf16)
 
             if i > 0:
-                send(ad, home, s, lambda: (total.at[i, :, half], r3.at[z, :, half]), column[i], got=z)
+                send(ad, home, s, lambda: (rr.at[i, :, half], r3.at[z, :, half]), column[i], got=z)
 
         when(ad, body)
         if i == 0:
             over = ad & (core != h)
-            when(over, lambda: send(over, "dp", h, lambda: (fin.at[h], out_ref), to_core))
+            when(over, lambda: send(over, "dp", h, lambda: (rr.at[0, :, half], out_ref), to_core))
 
     ops = {
         "sp": spread,
-        "gz": lambda i: (gather_z(i, ad), pass_z(i, ad)),
+        "gz": lambda i: (gather_z(i, ad), pass_z(i, ad, "tr" if i else "r")),
+        "tb": lambda i: (when(ad, table), spread_table(0), pass_z(0, ad, "t")),
         "gi": lambda i: (gather_z(i, ad & inner), pass_z(i, ad & inner)),
         "go": lambda i: gather_z(i, ad & outer),
+        "v0": plane_out, "v1": plane_on,
+        "za": lambda i: pass_v(i, 0), "zb": lambda i: (diagonal_in(i), pass_v(i, 1)),
+        "ra": lambda i: relay_v(i, 0), "rb": lambda i: relay_v(i, 1),
         "sy": share_y, "sx": share_x, "cf": forward,
         "ca": lambda i: backward(i, 0), "cb": lambda i: backward(i, 1),
         "1y": back1_y, "1x": back1_x,
@@ -328,7 +438,7 @@
         ops[name](i)
 
     def finish():
-        out_ref[...] = fin[core]
+        out_ref[...] = jnp.where(core == 0, rr[0, :, 0:cut], rr[0, :, cut:])
 
     when(ad, finish)
     when(bc, lambda: arrive("dp", core, out_ref, to_core))
@@ -349,7 +459,9 @@
     cap = capacity(experts, expert_ids.shape)
     cut, bf16, f32 = features // 2, jnp.bfloat16, jnp.float32
     vmem, hbm = pl.BlockSpec(memory_space=pltpu.VMEM), pl.BlockSpec(memory_space=pl.ANY)
-    count = 18 * planes
+    aside = put_aside(features)
+    near = (features - aside) // 2
+    count = 26 * planes
     return pl.pallas_call(
         functools.partial(kernel, cap),
         name="fused_backward",
@@ -357,13 +469,14 @@
         in_specs=[hbm] * 7,
         out_specs=vmem,
         scratch_shapes=[
-            pltpu.VMEM((planes, 2, rows, features), bf16),
+            pltpu.VMEM((planes, 2, rows, 2 * near), bf16),
+            pltpu.VMEM((planes, 2, 2, rows, aside), bf16),
             pltpu.VMEM((planes, 2, 2 * experts, rows), f32),
-            pltpu.VMEM((2, 2, 2, cap, cut), bf16),
+            pltpu.VMEM((2, 2, 2, cap, near), bf16),
+            pltpu.VMEM((planes - 1, 2, 2, cap, aside), bf16),
             pltpu.VMEM((planes, 2, 2 * cap, features), bf16),
             pltpu.VMEM((planes, 2 * cap, features), bf16),
             pltpu.VMEM((planes, cap, features), bf16),
-            pltpu.VMEM((planes, rows, features), bf16),
             pltpu.VMEM((planes, rows, features), bf16),
             pltpu.VMEM((planes, rows, features), bf16),
             pltpu.VMEM((planes, 2, 2 * cap, rows), bf16),
@@ -374,17 +487,20 @@
             pltpu.VMEM((planes, 2 * cap, hidden), bf16),
             pltpu.VMEM((planes, 2 * cap, hidden), bf16),
             pltpu.VMEM((planes, 2 * cap, 1), f32),
-            pltpu.VMEM((halves, rows, cut), bf16),
             pltpu.VMEM(expert_ids.shape, jnp.int32),
             pltpu.VMEM(gate_probs.shape, f32),
             pltpu.SemaphoreType.DMA((count,)),
             pltpu.SemaphoreType.DMA((count,)),
-            pltpu.SemaphoreType.DMA((7,)),
+            pltpu.SemaphoreType.DMA((9,)),
         ],
         compiler_params=pltpu.CompilerParams(
             collective_id=0, has_side_effects=True, vmem_limit_bytes=67043328
         ),
     )(layer_input, out_grad, expert_ids, gate_probs, gate_proj, up_proj, down_proj)
+
+
+def put_aside(features):
+    return 2 * features // 7 // 256 * 256
 
 
 def capacity(experts, shape):
@@ -429,9 +545,8 @@
     rows, features = args[0].shape
     hidden = args[4].shape[2]
     cap = capacity(experts, args[2].shape)
-    planes = experts // 4
-    held = 2 * features * (planes * (5 * rows + 7 * cap) + 3 * hidden + rows + 8 * cap)
-    fits = held < 64 * 10**6 and halves == 2 and experts == 16 and cap % 16 == 0
+    held = 2 * features * (LINE * (4 * rows + 7 * cap) + 3 * hidden + 6 * cap) + 16 * LINE * cap * hidden
+    fits = held < 66 * 10**6 and halves == 2 and experts == 4 * LINE and cap % 16 == 0
     return (fused if fits else dense)(*args)
 
 

time: 169 us -> 147 us (0.87); the launches traced: 167 us -> 147 us
  Pallas kernels: 162 us -> 143 us
    pallas_call x1, Pallas kernels: 162 us -> 143 us  [fused(): pl.pallas_call(functools.partial(kernel, cap), name='fused_backward', out...]
where the time goes in v3:
time: 147 us
  Pallas kernels  143 us (97%)
  local copies, waits for them, and re-layouts  4.63 us (3%)
    pallas_call x1, Pallas kernels, fused(): pl.pallas_call(functools.partial(kernel, cap), name='fused_backward', out...  143 us
    unnamed x3, local copies, waits for them, and re-layouts  4.63 us

profile of v3, /device:TPU:0, one launch (start us, length us, event | category | flops | bytes accessed | tf_op | source)
XLA Modules:
  0.0 147.2 jit_solution(13308115751978237958)
XLA Ops:
  0.0 1.4 copy.8.ids_hbm
  1.4 1.4 copy.9.prob_hbm
  2.8 142.6 %fused_backward.1 = bf16[128,1792]{1,0:T(8,128)(2,1)} custom-call(bf16[128,3584]{1,0:T(8,128)(2,1)} %x_hbm.1, bf16[128,3584]{1,0:T(8,128)(2,1)} %g_hbm.1, s32[128,8]{1,0:T(8,128)} %copy.8.ids_hbm, f32[128,8]{1,0:T(8,128)} %copy.9.prob_hbm, bf16[1,3584,1024]{2,1,0:T(8,128)(2,1)} %wg_hbm.1, bf16[1,3584,1024]{2,1,0:T(8,128)(2,1)} %wu_hbm.1, ...), custom_call_target="tpu_custom_call" | custom-call | tf_op jit(solution)/shard_map/fused_backward/pallas_call | solution.py:465
  145.4 1.8 %copy.11 = bf16[128,1792]{1,0:T(8,128)(2,1)} copy(bf16[128,1792]{1,0:T(8,128)(2,1)} %fused_backward.1) | data formatting | bytes 917504

commit v4 on v3

--- a/solution.py
+++ b/solution.py
@@ -123,19 +123,18 @@
     def table():
         for copy in own_lists():
             copy.wait()
-        name = lax.broadcasted_iota(jnp.int32, (rows, 128), 1)
-        count = jnp.zeros((rows, 128), f32)
-        prob = jnp.zeros((rows, 128), f32)
-        for k in range(ids_ref.shape[1]):
-            hit = ids_ref[:, k:k + 1] == name
+        name = lax.broadcasted_iota(jnp.int32, (experts, rows), 0)
+        count = jnp.zeros((experts, rows), f32)
+        prob = jnp.zeros((experts, rows), f32)
+        for k in range(ids_ref.shape[0]):
+            hit = ids_ref[k:k + 1, :] == name
             count = count + jnp.where(hit, 1.0, 0.0)
-            prob = prob + jnp.where(hit, prob_ref[:, k:k + 1], 0.0)
-        before = lax.broadcasted_iota(jnp.int32, (rows, rows), 1) < lax.broadcasted_iota(jnp.int32, (rows, rows), 0)
-        lower = jnp.where(before, 1.0, 0.0).astype(bf16)
-        rank = jnp.dot(lower, count.astype(bf16), preferred_element_type=f32)
-        code = jnp.where(count > 0.5, rank, -1.0)
-        tabs[z, 0, 0:experts, :] = code.T[0:experts]
-        tabs[z, 0, experts:, :] = prob.T[0:experts]
+            prob = prob + jnp.where(hit, prob_ref[k:k + 1, :], 0.0)
+        before = lax.broadcasted_iota(jnp.int32, (rows, rows), 0) < lax.broadcasted_iota(jnp.int32, (rows, rows), 1)
+        upper = jnp.where(before, 1.0, 0.0).astype(bf16)
+        rank = jnp.dot(count.astype(bf16), upper, preferred_element_type=f32)
+        tabs[z, 0, 0:experts, :] = jnp.where(count > 0.5, rank, -1.0)
+        tabs[z, 0, experts:, :] = prob
 
     def ready():
         for copy in own_copies():
@@ -487,8 +486,8 @@
             pltpu.VMEM((planes, 2 * cap, hidden), bf16),
             pltpu.VMEM((planes, 2 * cap, hidden), bf16),
             pltpu.VMEM((planes, 2 * cap, 1), f32),
-            pltpu.VMEM(expert_ids.shape, jnp.int32),
-            pltpu.VMEM(gate_probs.shape, f32),
+            pltpu.VMEM(expert_ids.shape[::-1], jnp.int32),
+            pltpu.VMEM(gate_probs.shape[::-1], f32),
             pltpu.SemaphoreType.DMA((count,)),
             pltpu.SemaphoreType.DMA((count,)),
             pltpu.SemaphoreType.DMA((9,)),
@@ -496,7 +495,7 @@
         compiler_params=pltpu.CompilerParams(
             collective_id=0, has_side_effects=True, vmem_limit_bytes=67043328
         ),
-    )(layer_input, out_grad, expert_ids, gate_probs, gate_proj, up_proj, down_proj)
+    )(layer_input, out_grad, expert_ids.T, gate_probs.T, gate_proj, up_proj, down_proj)
 
 
 def put_aside(features):

time: 147 us -> 144 us (0.980)
  local copies, waits for them, and re-layouts: 4.63 us -> 1.82 us
    unnamed x3 -> x1, local copies, waits for them, and re-layouts: 4.63 us -> 1.82 us
where the time goes in v4:
time: 144 us
  Pallas kernels  142 us (99%)
  local copies, waits for them, and re-layouts  1.82 us (1%)
    pallas_call x1, Pallas kernels, fused(): pl.pallas_call(functools.partial(kernel, cap), name='fused_backward', out...  142 us

profile of v4, /device:TPU:0, one launch (start us, length us, event | category | flops | bytes accessed | tf_op | source)
XLA Modules:
  0.0 144.3 jit_solution(16688690232463645804)
XLA Ops:
  0.0 142.4 %fused_backward.1 = bf16[128,1792]{1,0:T(8,128)(2,1)} custom-call(bf16[128,3584]{1,0:T(8,128)(2,1)} %x_hbm.1, bf16[128,3584]{1,0:T(8,128)(2,1)} %g_hbm.1, s32[8,128]{1,0:T(8,128)} %bitcast.2, f32[8,128]{1,0:T(8,128)} %bitcast.3, bf16[1,3584,1024]{2,1,0:T(8,128)(2,1)} %wg_hbm.1, bf16[1,3584,1024]{2,1,0:T(8,128)(2,1)} %wu_hbm.1, bf16[1,1024,3584]{2,1,0:T(8,128)(2,1)} %wd_hbm.1), custom_call_target="tpu_custom_call" | custom-call | tf_op jit(solution)/shard_map/fused_backward/pallas_call | solution.py:464
  142.5 1.8 %copy.9 = bf16[128,1792]{1,0:T(8,128)(2,1)} copy(bf16[128,1792]{1,0:T(8,128)(2,1)} %fused_backward.1) | data formatting | bytes 917504

commit v5 on v4

--- a/solution.py
+++ b/solution.py
@@ -338,7 +338,7 @@
             hit = slot == tabs[s, k, pl.ds(me, 1), :]
             pw[i, k * cap:(k + 1) * cap, :] = jnp.sum(
                 jnp.where(hit, tabs[s, k, pl.ds(experts + me, 1), :], 0.0), axis=1, keepdims=True)
-        tile = 256
+        tile = min(512, hidden)
 
         @pl.loop(0, hidden // tile)
         def _(f):

time: 144 us -> 144 us (level)
  no operation moved by 1% of the time
where the time goes in v5:
time: 144 us
  Pallas kernels  142 us (99%)
  local copies, waits for them, and re-layouts  1.82 us (1%)
    pallas_call x1, Pallas kernels, fused(): pl.pallas_call(functools.partial(kernel, cap), name='fused_backward', out...  142 us

profile of v5, /device:TPU:0, one launch (start us, length us, event | category | flops | bytes accessed | tf_op | source)
XLA Modules:
  0.0 144.1 jit_solution(3465570606102323250)
XLA Ops:
  0.0 142.3 %fused_backward.1 = bf16[128,1792]{1,0:T(8,128)(2,1)} custom-call(bf16[128,3584]{1,0:T(8,128)(2,1)} %x_hbm.1, bf16[128,3584]{1,0:T(8,128)(2,1)} %g_hbm.1, s32[8,128]{1,0:T(8,128)} %bitcast.2, f32[8,128]{1,0:T(8,128)} %bitcast.3, bf16[1,3584,1024]{2,1,0:T(8,128)(2,1)} %wg_hbm.1, bf16[1,3584,1024]{2,1,0:T(8,128)(2,1)} %wu_hbm.1, bf16[1,1024,3584]{2,1,0:T(8,128)(2,1)} %wd_hbm.1), custom_call_target="tpu_custom_call" | custom-call | tf_op jit(solution)/shard_map/fused_backward/pallas_call | solution.py:464
  142.3 1.8 %copy.9 = bf16[128,1792]{1,0:T(8,128)(2,1)} copy(bf16[128,1792]{1,0:T(8,128)(2,1)} %fused_backward.1) | data formatting | bytes 917504
